TPU v7x, 32 devices: a whole 2x2x4 slice. The times are simulated.
32 devices in a mesh: groups: 2 (over y), block: 4 (over z), seg: 2 (over x), sub: 2 (over core).
Axes of the slice: x: 2, y: 2, z: 4, core: 2. Of those that a mesh axis runs over, the one named last changes fastest.
Arguments:
- old_fields: float32 [2048, 4, 512], P(('groups', 'block', 'seg', 'sub')), parts along dimension 0, may hold values from -6 to 6
- corner_shift: float32 [24, 2048], P(None, ('groups', 'block', 'seg', 'sub')), parts along dimension 1, may hold values from -0.2 to 0.2
- targets: float32 [3, 131072], P(None, ('groups', 'block', 'seg', 'sub')), parts along dimension 1, may hold values from -0.7 to 0.7
- owners: int32 [1024], P(('groups', 'block', 'seg', 'sub')), parts along dimension 0, may hold values from 0 to 1023, as said below
Outputs:
- new_fields: float32 [4, 131072], P(None, ('groups', 'block', 'seg', 'sub')), parts along dimension 1
There are 2 independent parts, one for each index of `groups`. A program takes and returns all parts, laid end to end along the dimension named above; each array names one. Nothing has to cross between parts.
Inputs may be any that keep to these rules, and one draw needn't show every extreme that they name: `owners`: owner e lies on device e // 64. At most 2 of the blocks on the rows of one device are owned by elements of any one device, and in every draw some device owns exactly 2 blocks of every device.
All inputs are finite; a program needn't handle non-finite values.
Results may differ from a plain program's by a relative error of at most 0.00029.
Values sent between devices are 32-bit elements; how exact they have to be, the bound alone decides.
A program may use at most 64 MiB of HBM per device.

v0:
```python
import jax
import jax.numpy as jnp
import numpy as np
from jax import lax
from jax.sharding import PartitionSpec as P

NEWTON = 3
CAP = 2
GLL_POINTS = (
    -1.0,
    -0.8717401485096066,
    -0.5917001814331423,
    -0.2092992179024789,
    0.2092992179024789,
    0.5917001814331423,
    0.8717401485096066,
    1.0,
)
EXACT = lax.Precision.HIGHEST


def lagrange_rows(coords):
    gll_nodes = jnp.array(GLL_POINTS, jnp.float32)
    offsets = coords[None, :] - gll_nodes[:, None]
    spacing = gll_nodes[:, None] - gll_nodes[None, :] + jnp.eye(8, dtype=jnp.float32)
    diag_mask = jnp.eye(8, dtype=bool)
    factors = jnp.where(diag_mask[:, :, None], 1.0, offsets[None, :, :] / spacing[:, :, None])
    return jnp.prod(factors, axis=1)


def corner_signs():
    bit_table = np.array(
        [[corner >> 2 - coord_dim & 1 for corner in range(8)] for coord_dim in range(3)], np.float32
    )
    return jnp.asarray(2.0 * bit_table - 1.0)


def outer_prod(first, second, third):
    return (first[:, None, None, :] * second[None, :, None, :] * third[None, None, :, :]).reshape(
        8, -1
    )


def trilinear(ref_pos):
    shape_list = []
    slope_list = []
    for coord_dim in range(3):
        coordinate = ref_pos[coord_dim]
        shape_list.append(jnp.stack([0.5 - 0.5 * coordinate, 0.5 + 0.5 * coordinate]))
        slope_list.append(
            jnp.stack([jnp.full_like(coordinate, -0.5), jnp.full_like(coordinate, 0.5)])
        )
    values = outer_prod(shape_list[0], shape_list[1], shape_list[2])
    slopes = [
        outer_prod(slope_list[0], shape_list[1], shape_list[2]),
        outer_prod(shape_list[0], slope_list[1], shape_list[2]),
        outer_prod(shape_list[0], shape_list[1], slope_list[2]),
    ]
    return (values, slopes)


def solve_three(matrix, rhs_rows):
    cofactors = []
    for row_id in range(3):
        keep_rows = [remain for remain in range(3) if remain != row_id]
        cof_row = []
        for col_id in range(3):
            keep_cols = [remain for remain in range(3) if remain != col_id]
            sign_factor = 1.0 if (row_id + col_id) % 2 == 0 else -1.0
            cof_row.append(
                sign_factor
                * (
                    matrix[keep_rows[0]][keep_cols[0]] * matrix[keep_rows[1]][keep_cols[1]]
                    - matrix[keep_rows[0]][keep_cols[1]] * matrix[keep_rows[1]][keep_cols[0]]
                )
            )
        cofactors.append(cof_row)
    determinant = (
        matrix[0][0] * cofactors[0][0]
        + matrix[0][1] * cofactors[0][1]
        + matrix[0][2] * cofactors[0][2]
    )
    return [
        (
            cofactors[0][col_id] * rhs_rows[0]
            + cofactors[1][col_id] * rhs_rows[1]
            + cofactors[2][col_id] * rhs_rows[2]
        )
        / determinant
        for col_id in range(3)
    ]


def invert_map(corners, target):
    ref_pos = jnp.zeros_like(target)
    for iteration in range(NEWTON):
        values, slopes = trilinear(ref_pos)
        mapped = jnp.dot(corners, values, precision=EXACT)
        columns = [jnp.dot(corners, slope_row, precision=EXACT) for slope_row in slopes]
        matrix = [[columns[col_id][row_id] for col_id in range(3)] for row_id in range(3)]
        misfit = mapped - target
        update = solve_three(matrix, [misfit[row_id] for row_id in range(3)])
        ref_pos = jnp.clip(ref_pos - jnp.stack(update), -1.2, 1.2)
    return ref_pos


def interpolate(element_field, corners, target):
    ref_pos = invert_map(corners, target)
    along_x = lagrange_rows(ref_pos[0])
    along_y = lagrange_rows(ref_pos[1])
    along_z = lagrange_rows(ref_pos[2])
    weights = (along_y[:, None, :] * along_z[None, :, :]).reshape(64, -1)
    var_count = element_field.shape[0]
    partial_sum = jnp.dot(element_field.reshape(var_count * 8, 64), weights, precision=EXACT)
    return jnp.sum(partial_sum.reshape(var_count, 8, -1) * along_x[None, :, :], axis=1)


def interpolate_blocks(fields, shifts, points):
    cube_signs = corner_signs()

    def per_block(inputs):
        element_field, shift_row, target = inputs
        return interpolate(element_field, cube_signs + shift_row.reshape(3, 8), target)

    return lax.map(per_block, (fields, shifts, points), batch_size=64)


def slot_table(owners, elems_local, capacity):
    owner_dev = owners // elems_local
    local_elem = owners - owner_dev * elems_local
    block_count = owners.shape[0]
    earlier = jnp.tril(jnp.ones((block_count, block_count), jnp.int32), -1)
    matches = (owner_dev[:, None] == owner_dev[None, :]).astype(jnp.int32)
    arrival = jnp.sum(matches * earlier, axis=1)
    return (owner_dev * capacity + arrival, local_elem)


def shards(old_fields, corner_shift, targets, owners):
    outer_count = lax.axis_size("block")
    inner_count = lax.axis_size("seg") * lax.axis_size("sub")
    slot_count = outer_count * inner_count * CAP
    elems_local = old_fields.shape[0]
    var_count = old_fields.shape[1]
    block_count = owners.shape[0]
    slot_index, local_elem = slot_table(owners, elems_local, CAP)
    block_points = targets.reshape(3, block_count, -1).transpose(1, 0, 2)
    point_count = block_points.shape[2]
    outgoing = jnp.zeros((slot_count, 3, point_count), jnp.float32).at[slot_index].set(block_points)
    wanted = jnp.full((slot_count,), -1, jnp.int32).at[slot_index].set(local_elem)
    arrived, asked = (
        lax.all_to_all(
            lax.all_to_all(
                outgoing.reshape(outer_count, inner_count, CAP, 3, point_count),
                "block",
                split_axis=0,
                concat_axis=0,
                tiled=True,
            ),
            ("seg", "sub"),
            split_axis=1,
            concat_axis=1,
            tiled=True,
        ),
        lax.all_to_all(
            lax.all_to_all(
                wanted.reshape(outer_count, inner_count, CAP),
                "block",
                split_axis=0,
                concat_axis=0,
                tiled=True,
            ),
            ("seg", "sub"),
            split_axis=1,
            concat_axis=1,
            tiled=True,
        ),
    )
    asked = asked.reshape(slot_count)
    live_slot = asked >= 0
    element = jnp.where(live_slot, asked, 0)
    fields = old_fields[element]
    shifts = jnp.transpose(corner_shift[:, element])
    computed = interpolate_blocks(fields, shifts, arrived.reshape(slot_count, 3, point_count))
    computed = jnp.where(live_slot[:, None, None], computed, 0.0)
    returned = lax.all_to_all(
        lax.all_to_all(
            computed.reshape(outer_count, inner_count, CAP, var_count, point_count),
            "block",
            split_axis=0,
            concat_axis=0,
            tiled=True,
        ),
        ("seg", "sub"),
        split_axis=1,
        concat_axis=1,
        tiled=True,
    )
    mine = returned.reshape(slot_count, var_count, point_count)[slot_index]
    return mine.transpose(1, 0, 2).reshape(var_count, -1)


def solution(mesh):
    in_specs = (
        P(("groups", "block", "seg", "sub"), None, None),
        P(None, ("groups", "block", "seg", "sub")),
        P(None, ("groups", "block", "seg", "sub")),
        P(("groups", "block", "seg", "sub")),
    )
    out_specs = P(None, ("groups", "block", "seg", "sub"))
    return jax.shard_map(shards, mesh=mesh, in_specs=in_specs, out_specs=out_specs, check_vma=False)
```

profile of v0, /device:TPU:0, one launch (start us, length us, event | category | flops | bytes accessed | tf_op | source)
XLA Modules:
  0.0 64.6 jit_solution(12692678252523733216)
XLA Ops:
  0.0 0.7 %multiply_subtract_fusion.2 = (s32[32]{0:T(128)S(1)}, s32[32]{0:T(128)S(1)}, s32[32]{0:T(128)S(1)}) fusion(s32[32]{0:T(128)} %param.11), kind=kLoop, calls=%fused_computation.237 | loop fusion | flops 576 | bytes 512 | tf_op jit(solution)/shard_map/sub | solution.py:130
  0.7 0.2 select_reduce_fusion
  0.9 0.7 %scatter_custom_fusion = s32[32]{0:T(128)S(1)} fusion(s32[32]{0:T(128)S(1)} %compare_select_fusion.2, s32[32]{0:T(128)S(1)} %get-tuple-element.10, s32[]{:T(128)} %constant.26.clone.1), kind=kCustom, calls=%fused_computation.239 | custom fusion | bytes 132 | tf_op jit(solution)/shard_map/scatter | solution.py:149
  1.7 0.7 %copy.272 = s32[4,4,2]{1,2,0:T(2,128)} copy(s32[4,4,2]{2,1,0:T(4,128)S(1)} %reshape.2161) | data formatting | bytes 256 | tf_op jit(solution)/shard_map/reshape | solution.py:166
  2.4 6.5 %all-to-all-start = ((s32[4,4,2]{1,2,0:T(2,128)}), s32[4,4,2]{1,2,0:T(2,128)S(1)}, u32[]{:S(2)}, u32[]{:S(2)}) async-start(s32[4,4,2]{1,2,0:T(2,128)} %copy.272), calls=%async_computation | async-start | bytes 8192 | tf_op jit(solution)/shard_map/all_to_all | solution.py:165
  9.1 1.5 %scatter_fusion = f32[32,3,128]{2,1,0:T(4,128)S(1)} fusion(f32[32,3,128]{2,1,0:T(4,128)S(1)} %broadcast.569, s32[32]{0:T(128)S(1)} %compare_select_fusion.2, f32[32,3,128]{2,1,0:T(4,128)S(1)} %bitcast.790), kind=kCustom, calls=%fused_computation.4 | custom fusion | bytes 147584 | tf_op jit(solution)/shard_map/scatter | solution.py:148
  10.6 3.9 %all-to-all-done = s32[4,4,2]{1,2,0:T(2,128)S(1)} async-done(((s32[4,4,2]{1,2,0:T(2,128)}), s32[4,4,2]{1,2,0:T(2,128)S(1)}, u32[]{:S(2)}, u32[]{:S(2)}) %all-to-all-start) | async-done | bytes 160 | tf_op jit(solution)/shard_map/all_to_all | solution.py:165
  14.5 0.7 %copy.273 = s32[4,4,2]{0,2,1:T(2,128)} copy(s32[4,4,2]{1,2,0:T(2,128)S(1)} %all-to-all-done) | data formatting | bytes 256 | tf_op jit(solution)/shard_map/all_to_all | solution.py:165
  15.2 3.2 %all-to-all-start.1 = ((s32[4,4,2]{0,2,1:T(2,128)}), s32[4,4,2]{0,2,1:T(2,128)S(1)}, u32[]{:S(2)}, u32[]{:S(2)}) async-start(s32[4,4,2]{0,2,1:T(2,128)} %copy.273), calls=%async_computation.1 | async-start | bytes 8192 | tf_op jit(solution)/shard_map/all_to_all | solution.py:164
  18.4 0.6 %copy.281 = f32[4,4,2,3,128]{4,2,1,3,0:T(2,128)} copy(f32[4,4,2,3,128]{4,3,2,1,0:T(4,128)S(1)} %bitcast.767) | data formatting | bytes 98304 | tf_op jit(solution)/shard_map/reshape | solution.py:153
  19.1 3.1 %all-to-all-done.1 = s32[4,4,2]{0,2,1:T(2,128)S(1)} async-done(((s32[4,4,2]{0,2,1:T(2,128)}), s32[4,4,2]{0,2,1:T(2,128)S(1)}, u32[]{:S(2)}, u32[]{:S(2)}) %all-to-all-start.1) | async-done | bytes 160 | tf_op jit(solution)/shard_map/all_to_all | solution.py:164
  22.2 3.3 %all-to-all-start.2 = ((f32[4,4,2,3,128]{4,2,1,3,0:T(2,128)}), f32[4,4,2,3,128]{4,2,1,3,0:T(2,128)S(1)}, u32[]{:S(2)}, u32[]{:S(2)}) async-start(f32[4,4,2,3,128]{4,2,1,3,0:T(2,128)} %copy.281), calls=%async_computation.2 | async-start | bytes 98304 | tf_op jit(solution)/shard_map/all_to_all | solution.py:152
  25.5 0.1 copy.276
  25.6 0.1 reshape.2162
  25.7 0.6 gather_fusion.1
  26.3 0.6 copy-done.4
  26.9 0.7 %copy-done.6 = f32[24]{0:T(128)S(1)} copy-done((f32[24]{0:T(128)S(1)}, f32[24]{0:T(128)}, u32[]{:S(2)}) %copy-start.6) | copy-done | bytes 120
  27.6 0.3 fusion.91
  27.9 0.3 fusion.93
  28.3 0.3 fusion.95
  28.6 0.3 copy-done.5
  29.1 0.1 copy.274
  29.1 2.0 %all-to-all-done.2 = f32[4,4,2,3,128]{4,2,1,3,0:T(2,128)S(1)} async-done(((f32[4,4,2,3,128]{4,2,1,3,0:T(2,128)}), f32[4,4,2,3,128]{4,2,1,3,0:T(2,128)S(1)}, u32[]{:S(2)}, u32[]{:S(2)}) %all-to-all-start.2) | async-done | bytes 49184 | tf_op jit(solution)/shard_map/all_to_all | solution.py:152
  31.1 0.6 copy.282
  31.8 3.3 %all-to-all-start.3 = ((f32[4,4,2,3,128]{4,2,0,3,1:T(2,128)}), f32[4,4,2,3,128]{4,2,0,3,1:T(2,128)S(1)}, u32[]{:S(2)}, u32[]{:S(2)}) async-start(f32[4,4,2,3,128]{4,2,0,3,1:T(2,128)} %copy.282), calls=%async_computation.3 | async-start | bytes 98304 | tf_op jit(solution)/shard_map/all_to_all | solution.py:151
  35.2 0.7 %gather_fusion = f32[32,4,512]{2,1,0:T(4,128)S(1)} fusion(f32[64,4,512]{2,1,0:T(4,128)S(1)} %copy-done, s32[1024]{0:T(1024)S(1)} %pad_clamp_fusion.1), kind=kCustom, calls=%fused_computation | custom fusion | bytes 524416 | tf_op jit(solution)/shard_map/gather | solution.py:181
  35.9 0.2 reshape.2163
  36.1 0.1 copy.275
  36.2 2.8 %all-to-all-done.3 = f32[4,4,2,3,128]{4,2,0,3,1:T(2,128)S(1)} async-done(((f32[4,4,2,3,128]{4,2,0,3,1:T(2,128)}), f32[4,4,2,3,128]{4,2,0,3,1:T(2,128)S(1)}, u32[]{:S(2)}, u32[]{:S(2)}) %all-to-all-start.3) | async-done | bytes 49184 | tf_op jit(solution)/shard_map/all_to_all | solution.py:151
  39.1 0.3 convolution_subtract_fusion
  39.7 0.6 copy-done.2
  40.5 0.3 fusion.23
  40.9 0.3 fusion.17
  41.4 0.3 fusion.19
  41.7 0.3 fusion.21
  42.5 0.3 fusion.13
  42.9 0.3 fusion.11
  43.3 0.3 fusion.15
  43.7 0.3 fusion.9
  44.3 0.1 broadcast_add_fusion.2
  44.4 1.1 %fusion.4 = (f32[32,8,128]{2,1,0:T(8,128)S(1)}, f32[32,8,128]{2,1,0:T(8,128)S(1)}, f32[32,8,128]{2,1,0:T(8,128)S(1)}) fusion(f32[32,8,128]{2,1,0:T(8,128)S(1)} %get-tuple-element.61, f32[8,8]{1,0:T(8,128)S(1)} %add_add_fusion, pred[8,8]{1,0:T(8,128)(4,1)S(1)} %iota_compare_fusion.1, f32[32,8,128]{2,1,0:T(8,128)S(1)} %get-tuple-element.60, ...), kind=kLoop, calls=%fused_computation.14 | loop fusion | flops 2260992 | bytes 786752 | tf_op jit(solution)/shard_map/vmap()/reduce_prod | solution.py:28
  45.4 1.1 %fusion.1 = f32[32,4,128]{2,1,0:T(4,128)S(1)} fusion(f32[32,32,64]{2,1,0:T(8,128)S(1)} %reshape.2163, f32[32,8,128]{2,1,0:T(8,128)S(1)} %get-tuple-element.6, f32[32,8,128]{2,1,0:T(8,128)S(1)} %get-tuple-element.7, f32[32,8,128]{2,1,0:T(8,128)S(1)} %get-tuple-element.5), kind=kOutput, calls=%fused_computation.7 | convolution fusion | flops 101171200 | bytes 720896 | tf_op jit(solution)/shard_map/vmap()/dot_general | solution.py:114
  46.6 0.1 broadcast_select_fusion
  46.7 8.6 %all_to_all.30 = f32[4,4,2,4,128]{4,2,1,3,0:T(2,128)S(1)} all-to-all(f32[4,4,2,4,128]{4,2,1,3,0:T(2,128)S(1)} %copy.319), channel_id=1, replica_groups=mesh['groups'=2,'block'=4,'seg'=2,'sub'=2] {'block'}, dimensions={0} | all-to-all | bytes 131072 | tf_op jit(solution)/shard_map/all_to_all | solution.py:186
  55.3 0.6 %copy.320 = f32[4,4,2,4,128]{4,3,2,0,1:T(4,128)} copy(f32[4,4,2,4,128]{4,2,1,3,0:T(2,128)S(1)} %all_to_all.30) | data formatting | bytes 131072 | tf_op jit(solution)/shard_map/all_to_all | solution.py:186
  56.0 3.3 %all-to-all-start.5 = ((f32[4,4,2,4,128]{4,3,2,0,1:T(4,128)}), f32[4,4,2,4,128]{4,3,2,0,1:T(4,128)S(1)}, u32[]{:S(2)}, u32[]{:S(2)}) async-start(f32[4,4,2,4,128]{4,3,2,0,1:T(4,128)} %copy.320), calls=%async_computation.5 | async-start | bytes 131072 | tf_op jit(solution)/shard_map/all_to_all | solution.py:185
  59.3 4.1 %all-to-all-done.5 = f32[4,4,2,4,128]{4,3,2,0,1:T(4,128)S(1)} async-done(((f32[4,4,2,4,128]{4,3,2,0,1:T(4,128)}), f32[4,4,2,4,128]{4,3,2,0,1:T(4,128)S(1)}, u32[]{:S(2)}, u32[]{:S(2)}) %all-to-all-start.5) | async-done | bytes 65568 | tf_op jit(solution)/shard_map/all_to_all | solution.py:185
  63.4 1.2 %gather_fusion.2 = f32[32,4,128]{2,1,0:T(4,128)} fusion(f32[32,4,128]{2,1,0:T(4,128)S(1)} %bitcast.769, s32[1024]{0:T(1024)S(1)} %pad_clamp_fusion), kind=kCustom, calls=%fused_computation.2 | custom fusion | bytes 131200 | tf_op jit(solution)/shard_map/gather | solution.py:198
  (75 shorter events, 1.7 us)
Async XLA Ops:
  0.0 35.1 %copy-start = (f32[64,4,512]{2,1,0:T(4,128)S(1)}, f32[64,4,512]{2,1,0:T(4,128)}, u32[]{:S(2)}) copy-start(f32[64,4,512]{2,1,0:T(4,128)} %param.8) | copy-start | bytes 1572868
  1.7 7.2 %copy-start.3 = (f32[24,64]{1,0:T(8,128)S(1)}, f32[24,64]{1,0:T(8,128)}, u32[]{:S(2)}) copy-start(f32[24,64]{1,0:T(8,128)} %param.9) | copy-start | bytes 18436
  1.7 7.3 %copy-start.7 = (f32[8]{0:T(128)S(1)}, f32[8]{0:T(128)}, u32[]{:S(2)}) copy-start(f32[8]{0:T(128)} %constant.77) | copy-start | bytes 100
  1.7 7.3 %copy-start.8 = (f32[8]{0:T(128)S(1)}, f32[8]{0:T(128)}, u32[]{:S(2)}) copy-start(f32[8]{0:T(128)} %constant.75.clone) | copy-start | bytes 100
  2.4 6.7 %copy-start.1 = (f32[3,4096]{1,0:T(4,128)S(1)}, f32[3,4096]{1,0:T(4,128)}, u32[]{:S(2)}) copy-start(f32[3,4096]{1,0:T(4,128)} %param.10) | copy-start | bytes 147460
  2.4 12.1 %all-to-all-start = ((s32[4,4,2]{1,2,0:T(2,128)}), s32[4,4,2]{1,2,0:T(2,128)S(1)}, u32[]{:S(2)}, u32[]{:S(2)}) async-start(s32[4,4,2]{1,2,0:T(2,128)} %copy.272), calls=%async_computation | async-start | bytes 8192 | tf_op jit(solution)/shard_map/all_to_all | solution.py:165
  15.2 7.0 %all-to-all-start.1 = ((s32[4,4,2]{0,2,1:T(2,128)}), s32[4,4,2]{0,2,1:T(2,128)S(1)}, u32[]{:S(2)}, u32[]{:S(2)}) async-start(s32[4,4,2]{0,2,1:T(2,128)} %copy.273), calls=%async_computation.1 | async-start | bytes 8192 | tf_op jit(solution)/shard_map/all_to_all | solution.py:164
  22.2 8.9 %all-to-all-start.2 = ((f32[4,4,2,3,128]{4,2,1,3,0:T(2,128)}), f32[4,4,2,3,128]{4,2,1,3,0:T(2,128)S(1)}, u32[]{:S(2)}, u32[]{:S(2)}) async-start(f32[4,4,2,3,128]{4,2,1,3,0:T(2,128)} %copy.281), calls=%async_computation.2 | async-start | bytes 98304 | tf_op jit(solution)/shard_map/all_to_all | solution.py:152
  26.3 0.7 %copy-start.4 = (f32[2,128]{1,0:T(2,128)S(1)}, f32[2,128]{1,0:T(2,128)}, u32[]{:S(2)}) copy-start(f32[2,128]{1,0:T(2,128)} %constant.68.clone.1) | copy-start | bytes 3076
  26.9 0.7 %copy-start.6 = (f32[24]{0:T(128)S(1)}, f32[24]{0:T(128)}, u32[]{:S(2)}) copy-start(f32[24]{0:T(128)} %constant.76) | copy-start | bytes 292
  28.3 0.7 %copy-start.5 = (f32[3,8]{1,0:T(4,128)S(1)}, f32[3,8]{1,0:T(4,128)}, u32[]{:S(2)}) copy-start(f32[3,8]{1,0:T(4,128)} %constant.74.clone) | copy-start | bytes 292
  31.8 7.3 %all-to-all-start.3 = ((f32[4,4,2,3,128]{4,2,0,3,1:T(2,128)}), f32[4,4,2,3,128]{4,2,0,3,1:T(2,128)S(1)}, u32[]{:S(2)}, u32[]{:S(2)}) async-start(f32[4,4,2,3,128]{4,2,0,3,1:T(2,128)} %copy.282), calls=%async_computation.3 | async-start | bytes 98304 | tf_op jit(solution)/shard_map/all_to_all | solution.py:151
  39.6 0.7 %copy-start.2 = (f32[2,128]{1,0:T(2,128)S(1)}, f32[2,128]{1,0:T(2,128)}, u32[]{:S(2)}) copy-start(f32[2,128]{1,0:T(2,128)} %constant.73.clone.1) | copy-start | bytes 3076
  56.0 7.4 %all-to-all-start.5 = ((f32[4,4,2,4,128]{4,3,2,0,1:T(4,128)}), f32[4,4,2,4,128]{4,3,2,0,1:T(4,128)S(1)}, u32[]{:S(2)}, u32[]{:S(2)}) async-start(f32[4,4,2,4,128]{4,3,2,0,1:T(4,128)} %copy.320), calls=%async_computation.5 | async-start | bytes 131072 | tf_op jit(solution)/shard_map/all_to_all | solution.py:185
where the time goes:
time: 65.3 us; the launch traced here: 64.6 us
  starting transfers between devices  19.6 us (30%)
  waiting for transfers between devices  15.9 us (24%)
  local copies, waits for them, and re-layouts  12 us (18%)
  blocking collectives  8.63 us (13%)
  matrix products  5.16 us (8%)
  other arithmetic  2.71 us (4%)
    all_to_all x1, blocking collectives, shards(): lax.all_to_all(computed.reshape(outer_count, inner_count, CAP, var_count,...  8.63 us
    all_to_all x1, starting transfers between devices, shards(): lax.all_to_all(wanted.reshape(outer_count, inner_count, CAP), 'block', sp...  6.48 us
    all_to_all x1, waiting for transfers between devices, shards(): lax.all_to_all(lax.all_to_all(computed.reshape(outer_count, inner_count,...  4.07 us
    all_to_all x1, waiting for transfers between devices, shards(): lax.all_to_all(wanted.reshape(outer_count, inner_count, CAP), 'block', sp...  3.88 us
    all_to_all x1, starting transfers between devices, shards(): lax.all_to_all(lax.all_to_all(computed.reshape(outer_count, inner_count,...  3.28 us
    all_to_all x1, starting transfers between devices, shards(): lax.all_to_all(outgoing.reshape(outer_count, inner_count, CAP, 3, point_c...  3.27 us
    all_to_all x1, starting transfers between devices, shards(): lax.all_to_all(lax.all_to_all(outgoing.reshape(outer_count, inner_count,...  3.27 us
    all_to_all x1, starting transfers between devices, shards(): lax.all_to_all(lax.all_to_all(wanted.reshape(outer_count, inner_count, CA...  3.24 us
  transfers between devices with their start and end apart: 5, of which 5 were waited for; matrix products, arithmetic and copies ran while one was open for 8% of the time, Pallas kernels for 0%

commit v1 on v0

--- a/solution.py
+++ b/solution.py
@@ -17,6 +17,40 @@
     1.0,
 )
 EXACT = lax.Precision.HIGHEST
+
+
+def samples_all_track(my_data, which_dim, u_in):
+    a_next, t1 = (my_data.shape[:which_dim], my_data.shape[which_dim + 1 :])
+    seen_now = my_data.reshape(*a_next, u_in, -1, *t1)
+    view_out = jnp.moveaxis(seen_now, which_dim, 0)
+    return view_out
+
+
+def connect_grid(unit, array_axis):
+    unit = jnp.moveaxis(unit, 0, array_axis)
+    state_now = unit.shape
+    arr_out = unit.reshape(
+        *state_now[:array_axis],
+        state_now[array_axis] * state_now[array_axis + 1],
+        *state_now[array_axis + 2 :]
+    )
+    return arr_out
+
+
+def end_screen(raw, dev_axis, x_in, m):
+    formed = jax.lax.axis_index(dev_axis)
+    local_part = jax.lax.axis_size(dev_axis)
+    extra, e_next = (local_part, formed)
+    k_now = samples_all_track(raw, x_in, extra)
+    heap = [k_now[e_next]]
+    for w in [*range(1, extra)]:
+        y1 = k_now[e_next ^ w]
+        near = jax.lax.ppermute(y1, dev_axis, perm=[(dev_i, dev_i ^ w) for dev_i in range(extra)])
+        heap.append(near)
+    raw_out = jnp.stack(heap)
+    k_now = raw_out[e_next ^ jnp.arange(extra)]
+    opened = connect_grid(k_now, m)
+    return opened
 
 
 def lagrange_rows(coords):
@@ -182,7 +216,7 @@
     shifts = jnp.transpose(corner_shift[:, element])
     computed = interpolate_blocks(fields, shifts, arrived.reshape(slot_count, 3, point_count))
     computed = jnp.where(live_slot[:, None, None], computed, 0.0)
-    returned = lax.all_to_all(
+    returned = end_screen(
         lax.all_to_all(
             computed.reshape(outer_count, inner_count, CAP, var_count, point_count),
             "block",
@@ -191,9 +225,8 @@
             tiled=True,
         ),
         ("seg", "sub"),
-        split_axis=1,
-        concat_axis=1,
-        tiled=True,
+        1,
+        1,
     )
     mine = returned.reshape(slot_count, var_count, point_count)[slot_index]
     return mine.transpose(1, 0, 2).reshape(var_count, -1)

time: 65.3 us -> 62.7 us (0.960)
  blocking collectives: 8.63 us -> 0 us
  waiting for transfers between devices: 15.9 us -> 18.7 us
  starting transfers between devices: 19.6 us -> 21.3 us
  local copies, waits for them, and re-layouts: 12 us -> 13.4 us
    all_to_all x1 -> x0, blocking collectives: 8.63 us -> none  [shards(): lax.all_to_all(computed.reshape(outer_count, inner_count, CAP, var_count,...]
    ppermute x0 -> x3, waiting for transfers between devices: none -> 1.95 us  [end_screen(): jax.lax.ppermute(y1, dev_axis, perm=[(dev_i, dev_i ^ w) for dev_i in rang...]
    ppermute x0 -> x3, starting transfers between devices: none -> 1.92 us  [end_screen(): jax.lax.ppermute(y1, dev_axis, perm=[(dev_i, dev_i ^ w) for dev_i in rang...]
    all_to_all x1, waiting for transfers between devices: 4.07 us -> 5.7 us  [shards(): lax.all_to_all(computed.reshape(outer_count, inner_count, CAP, var_count,...]
    all_to_all x1, waiting for transfers between devices: 3.88 us -> 2.47 us  [shards(): lax.all_to_all(wanted.reshape(outer_count, inner_count, CAP), 'block', sp...]
    unnamed x19, local copies, waits for them, and re-layouts: 2.35 us -> 3.06 us
    select_n x1, local copies, waits for them, and re-layouts: 0.01 us -> 0.67 us  [shards(): computed = jnp.where(live_slot[:, None, None], computed, 0.0)]
  transfers between devices with their start and end apart: 5 -> 8, of which waited for: 5 -> 6; matrix products, arithmetic and copies ran while one was open for 8% -> 9% of each run, Pallas kernels for 0% -> 0%
where the time goes in v1:
time: 62.7 us; the launch traced here: 62 us
  starting transfers between devices  21.3 us (34%)
  waiting for transfers between devices  18.7 us (30%)
  local copies, waits for them, and re-layouts  13.4 us (21%)
  matrix products  5.16 us (8%)
  other arithmetic  2.74 us (4%)
  between operations  0.68 us (1%)
    all_to_all x1, starting transfers between devices, shards(): lax.all_to_all(wanted.reshape(outer_count, inner_count, CAP), 'block', sp...  6.35 us
    all_to_all x1, waiting for transfers between devices, shards(): lax.all_to_all(computed.reshape(outer_count, inner_count, CAP, var_count,...  5.7 us
    all_to_all x1, waiting for transfers between devices, shards(): lax.all_to_all(lax.all_to_all(wanted.reshape(outer_count, inner_count, CA...  3.76 us
    all_to_all x1, starting transfers between devices, shards(): lax.all_to_all(computed.reshape(outer_count, inner_count, CAP, var_count,...  3.28 us
    all_to_all x1, starting transfers between devices, shards(): lax.all_to_all(outgoing.reshape(outer_count, inner_count, CAP, 3, point_c...  3.27 us
    all_to_all x1, starting transfers between devices, shards(): lax.all_to_all(lax.all_to_all(outgoing.reshape(outer_count, inner_count,...  3.27 us
    all_to_all x1, starting transfers between devices, shards(): lax.all_to_all(lax.all_to_all(wanted.reshape(outer_count, inner_count, CA...  3.2 us
    unnamed x19, local copies, waits for them, and re-layouts  3.06 us
  transfers between devices with their start and end apart: 8, of which 6 were waited for; matrix products, arithmetic and copies ran while one was open for 9% of the time, Pallas kernels for 0%

profile of v1, /device:TPU:0, one launch (start us, length us, event | category | flops | bytes accessed | tf_op | source)
XLA Modules:
  0.0 62.0 jit_solution(17651697479478082455)
XLA Ops:
  0.0 0.7 %multiply_subtract_fusion.2 = (s32[32]{0:T(128)S(1)}, s32[32]{0:T(128)S(1)}, s32[32]{0:T(128)S(1)}) fusion(s32[32]{0:T(128)} %param.11), kind=kLoop, calls=%fused_computation.246 | loop fusion | flops 576 | bytes 512 | tf_op jit(solution)/shard_map/sub | solution.py:164
  0.7 0.2 select_reduce_fusion
  0.9 0.7 %scatter_custom_fusion = s32[32]{0:T(128)S(1)} fusion(s32[32]{0:T(128)S(1)} %compare_select_fusion.3, s32[32]{0:T(128)S(1)} %get-tuple-element.10, s32[]{:T(128)} %constant.29.clone.1), kind=kCustom, calls=%fused_computation.248 | custom fusion | bytes 132 | tf_op jit(solution)/shard_map/scatter | solution.py:183
  1.7 0.7 %copy.279 = s32[4,4,2]{1,2,0:T(2,128)} copy(s32[4,4,2]{2,1,0:T(4,128)S(1)} %reshape.2190) | data formatting | bytes 256 | tf_op jit(solution)/shard_map/reshape | solution.py:200
  2.4 6.3 %all-to-all-start = ((s32[4,4,2]{1,2,0:T(2,128)}), s32[4,4,2]{1,2,0:T(2,128)S(1)}, u32[]{:S(2)}, u32[]{:S(2)}) async-start(s32[4,4,2]{1,2,0:T(2,128)} %copy.279), calls=%async_computation | async-start | bytes 8192 | tf_op jit(solution)/shard_map/all_to_all | solution.py:199
  8.8 0.7 %copy-done.3 = f32[24,64]{1,0:T(8,128)S(1)} copy-done((f32[24,64]{1,0:T(8,128)S(1)}, f32[24,64]{1,0:T(8,128)}, u32[]{:S(2)}) %copy-start.3) | copy-done | bytes 6168
  9.6 1.5 %scatter_fusion = f32[32,3,128]{2,1,0:T(4,128)S(1)} fusion(f32[32,3,128]{2,1,0:T(4,128)S(1)} %broadcast.596, s32[32]{0:T(128)S(1)} %compare_select_fusion.3, f32[32,3,128]{2,1,0:T(4,128)S(1)} %bitcast.809), kind=kCustom, calls=%fused_computation.5 | custom fusion | bytes 147584 | tf_op jit(solution)/shard_map/scatter | solution.py:182
  11.1 0.6 %copy.288 = f32[4,4,2,3,128]{4,2,1,3,0:T(2,128)} copy(f32[4,4,2,3,128]{4,3,2,1,0:T(4,128)S(1)} %bitcast.785) | data formatting | bytes 98304 | tf_op jit(solution)/shard_map/reshape | solution.py:187
  11.9 2.5 %all-to-all-done = s32[4,4,2]{1,2,0:T(2,128)S(1)} async-done(((s32[4,4,2]{1,2,0:T(2,128)}), s32[4,4,2]{1,2,0:T(2,128)S(1)}, u32[]{:S(2)}, u32[]{:S(2)}) %all-to-all-start) | async-done | bytes 160 | tf_op jit(solution)/shard_map/all_to_all | solution.py:199
  14.3 0.7 %copy.280 = s32[4,4,2]{0,2,1:T(2,128)} copy(s32[4,4,2]{1,2,0:T(2,128)S(1)} %all-to-all-done) | data formatting | bytes 256 | tf_op jit(solution)/shard_map/all_to_all | solution.py:199
  15.0 3.2 %all-to-all-start.1 = ((s32[4,4,2]{0,2,1:T(2,128)}), s32[4,4,2]{0,2,1:T(2,128)S(1)}, u32[]{:S(2)}, u32[]{:S(2)}) async-start(s32[4,4,2]{0,2,1:T(2,128)} %copy.280), calls=%async_computation.1 | async-start | bytes 8192 | tf_op jit(solution)/shard_map/all_to_all | solution.py:198
  18.2 3.8 %all-to-all-done.1 = s32[4,4,2]{0,2,1:T(2,128)S(1)} async-done(((s32[4,4,2]{0,2,1:T(2,128)}), s32[4,4,2]{0,2,1:T(2,128)S(1)}, u32[]{:S(2)}, u32[]{:S(2)}) %all-to-all-start.1) | async-done | bytes 160 | tf_op jit(solution)/shard_map/all_to_all | solution.py:198
  22.0 3.3 %all-to-all-start.2 = ((f32[4,4,2,3,128]{4,2,1,3,0:T(2,128)}), f32[4,4,2,3,128]{4,2,1,3,0:T(2,128)S(1)}, u32[]{:S(2)}, u32[]{:S(2)}) async-start(f32[4,4,2,3,128]{4,2,1,3,0:T(2,128)} %copy.288), calls=%async_computation.2 | async-start | bytes 98304 | tf_op jit(solution)/shard_map/all_to_all | solution.py:186
  25.3 0.1 copy.283
  25.5 0.6 gather_fusion.1
  26.1 0.6 copy-done.4
  26.8 0.7 %copy-done.6 = f32[24]{0:T(128)S(1)} copy-done((f32[24]{0:T(128)S(1)}, f32[24]{0:T(128)}, u32[]{:S(2)}) %copy-start.6) | copy-done | bytes 120
  27.4 0.3 fusion.91
  27.8 0.3 fusion.93
  28.1 0.3 fusion.95
  28.4 0.3 copy-done.5
  29.0 2.0 %all-to-all-done.2 = f32[4,4,2,3,128]{4,2,1,3,0:T(2,128)S(1)} async-done(((f32[4,4,2,3,128]{4,2,1,3,0:T(2,128)}), f32[4,4,2,3,128]{4,2,1,3,0:T(2,128)S(1)}, u32[]{:S(2)}, u32[]{:S(2)}) %all-to-all-start.2) | async-done | bytes 49184 | tf_op jit(solution)/shard_map/all_to_all | solution.py:186
  30.9 0.6 %copy.289 = f32[4,4,2,3,128]{4,2,0,3,1:T(2,128)} copy(f32[4,4,2,3,128]{4,2,1,3,0:T(2,128)S(1)} %all-to-all-done.2) | data formatting | bytes 98304 | tf_op jit(solution)/shard_map/all_to_all | solution.py:186
  31.6 3.3 %all-to-all-start.3 = ((f32[4,4,2,3,128]{4,2,0,3,1:T(2,128)}), f32[4,4,2,3,128]{4,2,0,3,1:T(2,128)S(1)}, u32[]{:S(2)}, u32[]{:S(2)}) async-start(f32[4,4,2,3,128]{4,2,0,3,1:T(2,128)} %copy.289), calls=%async_computation.3 | async-start | bytes 98304 | tf_op jit(solution)/shard_map/all_to_all | solution.py:185
  35.0 0.7 %gather_fusion = f32[32,4,512]{2,1,0:T(4,128)S(1)} fusion(f32[64,4,512]{2,1,0:T(4,128)S(1)} %copy-done, s32[1024]{0:T(1024)S(1)} %pad_clamp_fusion.2), kind=kCustom, calls=%fused_computation | custom fusion | bytes 524416 | tf_op jit(solution)/shard_map/gather | solution.py:215
  35.7 0.2 reshape.2192
  35.9 0.1 copy.282
  36.0 2.8 %all-to-all-done.3 = f32[4,4,2,3,128]{4,2,0,3,1:T(2,128)S(1)} async-done(((f32[4,4,2,3,128]{4,2,0,3,1:T(2,128)}), f32[4,4,2,3,128]{4,2,0,3,1:T(2,128)S(1)}, u32[]{:S(2)}, u32[]{:S(2)}) %all-to-all-start.3) | async-done | bytes 49184 | tf_op jit(solution)/shard_map/all_to_all | solution.py:185
  38.9 0.3 convolution_subtract_fusion
  39.5 0.6 %copy-done.2 = f32[2,128]{1,0:T(2,128)S(1)} copy-done((f32[2,128]{1,0:T(2,128)S(1)}, f32[2,128]{1,0:T(2,128)}, u32[]{:S(2)}) %copy-start.2) | copy-done | bytes 1048
  40.3 0.3 fusion.23
  40.7 0.3 fusion.17
  41.2 0.3 fusion.19
  41.5 0.3 fusion.21
  42.3 0.3 fusion.13
  42.7 0.3 fusion.11
  43.1 0.3 fusion.15
  43.5 0.3 fusion.9
  44.2 1.1 %fusion.4 = (f32[32,8,128]{2,1,0:T(8,128)S(1)}, f32[32,8,128]{2,1,0:T(8,128)S(1)}, f32[32,8,128]{2,1,0:T(8,128)S(1)}) fusion(f32[32,8,128]{2,1,0:T(8,128)S(1)} %get-tuple-element.65, f32[8,8]{1,0:T(8,128)S(1)} %add_add_fusion, pred[8,8]{1,0:T(8,128)(4,1)S(1)} %iota_compare_fusion.1, f32[32,8,128]{2,1,0:T(8,128)S(1)} %get-tuple-element.64, ...), kind=kLoop, calls=%fused_computation.15 | loop fusion | flops 2260992 | bytes 786752 | tf_op jit(solution)/shard_map/vmap()/reduce_prod | solution.py:62
  45.2 1.1 %fusion.1 = f32[32,4,128]{2,1,0:T(4,128)S(1)} fusion(f32[32,32,64]{2,1,0:T(8,128)S(1)} %reshape.2192, f32[32,8,128]{2,1,0:T(8,128)S(1)} %get-tuple-element.6, f32[32,8,128]{2,1,0:T(8,128)S(1)} %get-tuple-element.7, f32[32,8,128]{2,1,0:T(8,128)S(1)} %get-tuple-element.5), kind=kOutput, calls=%fused_computation.8 | convolution fusion | flops 101171200 | bytes 720896 | tf_op jit(solution)/shard_map/vmap()/dot_general | solution.py:148
  46.5 0.7 %copy.326 = f32[4,4,2,4,128]{4,3,2,1,0:T(4,128)} copy(f32[4,4,2,4,128]{4,2,1,0,3:T(2,128)S(1)} %broadcast_select_fusion) | data formatting | bytes 131072 | tf_op jit(solution)/shard_map/jit(_where)/select_n | solution.py:218
  47.2 3.3 %all-to-all-start.4 = ((f32[4,4,2,4,128]{4,3,2,1,0:T(4,128)}), f32[4,4,2,4,128]{4,3,2,1,0:T(4,128)S(1)}, u32[]{:S(2)}, u32[]{:S(2)}) async-start(f32[4,4,2,4,128]{4,3,2,1,0:T(4,128)} %copy.326), calls=%async_computation.4 | async-start | bytes 131072 | tf_op jit(solution)/shard_map/all_to_all | solution.py:220
  50.5 5.7 %all-to-all-done.4 = f32[4,4,2,4,128]{4,3,2,1,0:T(4,128)S(1)} async-done(((f32[4,4,2,4,128]{4,3,2,1,0:T(4,128)}), f32[4,4,2,4,128]{4,3,2,1,0:T(4,128)S(1)}, u32[]{:S(2)}, u32[]{:S(2)}) %all-to-all-start.4) | async-done | bytes 65568 | tf_op jit(solution)/shard_map/all_to_all | solution.py:220
  56.3 0.1 collective-permute-start.1
  56.4 1.7 %collective-permute-start.2 = (f32[4,1,2,4,128]{4,3,2,0,1:T(4,128)S(1)}, f32[4,1,2,4,128]{4,3,2,0,1:T(4,128)S(1)}, u32[]{:S(2)}, u32[]{:S(2)}) collective-permute-start(f32[4,1,2,4,128]{4,3,2,0,1:T(4,128)S(1)} %get-tuple-element.23), channel_id=1, source_target_pairs={{0,3},{1,2},{2,1},{3,0},{4,7},{5,6},{6,5},{7,4},{8,11},{9,10},{10,... | collective-permute-start | bytes 49160 | tf_op jit(solution)/shard_map/ppermute | solution.py:48
  58.1 1.9 %collective-permute-done.1 = f32[4,1,2,4,128]{4,3,2,0,1:T(4,128)S(1)} collective-permute-done((f32[4,1,2,4,128]{4,3,2,0,1:T(4,128)S(1)}, f32[4,1,2,4,128]{4,3,2,0,1:T(4,128)S(1)}, u32[]{:S(2)}, u32[]{:S(2)}) %collective-permute-start.1) | collective-permute-done | bytes 16416 | tf_op jit(solution)/shard_map/ppermute | solution.py:48
  60.1 0.6 gather_fusion.2
  60.8 1.2 %gather_fusion.3 = f32[32,4,128]{2,1,0:T(4,128)} fusion(f32[32,4,128]{2,1,0:T(4,128)S(1)} %copy.331, s32[1024]{0:T(1024)S(1)} %pad_clamp_fusion), kind=kCustom, calls=%fused_computation.3 | custom fusion | bytes 131200 | tf_op jit(solution)/shard_map/gather | solution.py:231
  (85 shorter events, 2.3 us)
Async XLA Ops:
  0.0 35.0 %copy-start = (f32[64,4,512]{2,1,0:T(4,128)S(1)}, f32[64,4,512]{2,1,0:T(4,128)}, u32[]{:S(2)}) copy-start(f32[64,4,512]{2,1,0:T(4,128)} %param.8) | copy-start | bytes 1572868
  2.4 11.9 %all-to-all-start = ((s32[4,4,2]{1,2,0:T(2,128)}), s32[4,4,2]{1,2,0:T(2,128)S(1)}, u32[]{:S(2)}, u32[]{:S(2)}) async-start(s32[4,4,2]{1,2,0:T(2,128)} %copy.279), calls=%async_computation | async-start | bytes 8192 | tf_op jit(solution)/shard_map/all_to_all | solution.py:199
  8.8 0.7 %copy-start.3 = (f32[24,64]{1,0:T(8,128)S(1)}, f32[24,64]{1,0:T(8,128)}, u32[]{:S(2)}) copy-start(f32[24,64]{1,0:T(8,128)} %param.9) | copy-start | bytes 18436
  8.8 0.8 %copy-start.1 = (f32[3,4096]{1,0:T(4,128)S(1)}, f32[3,4096]{1,0:T(4,128)}, u32[]{:S(2)}) copy-start(f32[3,4096]{1,0:T(4,128)} %param.10) | copy-start | bytes 147460
  11.1 0.7 %copy-start.7 = (f32[8]{0:T(128)S(1)}, f32[8]{0:T(128)}, u32[]{:S(2)}) copy-start(f32[8]{0:T(128)} %constant.91) | copy-start | bytes 100
  11.1 0.7 %copy-start.8 = (f32[8]{0:T(128)S(1)}, f32[8]{0:T(128)}, u32[]{:S(2)}) copy-start(f32[8]{0:T(128)} %constant.89.clone) | copy-start | bytes 100
  15.0 7.0 %all-to-all-start.1 = ((s32[4,4,2]{0,2,1:T(2,128)}), s32[4,4,2]{0,2,1:T(2,128)S(1)}, u32[]{:S(2)}, u32[]{:S(2)}) async-start(s32[4,4,2]{0,2,1:T(2,128)} %copy.280), calls=%async_computation.1 | async-start | bytes 8192 | tf_op jit(solution)/shard_map/all_to_all | solution.py:198
  22.0 8.9 %all-to-all-start.2 = ((f32[4,4,2,3,128]{4,2,1,3,0:T(2,128)}), f32[4,4,2,3,128]{4,2,1,3,0:T(2,128)S(1)}, u32[]{:S(2)}, u32[]{:S(2)}) async-start(f32[4,4,2,3,128]{4,2,1,3,0:T(2,128)} %copy.288), calls=%async_computation.2 | async-start | bytes 98304 | tf_op jit(solution)/shard_map/all_to_all | solution.py:186
  26.1 0.7 %copy-start.4 = (f32[2,128]{1,0:T(2,128)S(1)}, f32[2,128]{1,0:T(2,128)}, u32[]{:S(2)}) copy-start(f32[2,128]{1,0:T(2,128)} %constant.79.clone.1) | copy-start | bytes 3076
  26.8 0.7 %copy-start.6 = (f32[24]{0:T(128)S(1)}, f32[24]{0:T(128)}, u32[]{:S(2)}) copy-start(f32[24]{0:T(128)} %constant.90) | copy-start | bytes 292
  28.1 0.7 %copy-start.5 = (f32[3,8]{1,0:T(4,128)S(1)}, f32[3,8]{1,0:T(4,128)}, u32[]{:S(2)}) copy-start(f32[3,8]{1,0:T(4,128)} %constant.88.clone) | copy-start | bytes 292
  31.6 7.3 %all-to-all-start.3 = ((f32[4,4,2,3,128]{4,2,0,3,1:T(2,128)}), f32[4,4,2,3,128]{4,2,0,3,1:T(2,128)S(1)}, u32[]{:S(2)}, u32[]{:S(2)}) async-start(f32[4,4,2,3,128]{4,2,0,3,1:T(2,128)} %copy.289), calls=%async_computation.3 | async-start | bytes 98304 | tf_op jit(solution)/shard_map/all_to_all | solution.py:185
  39.4 0.7 %copy-start.2 = (f32[2,128]{1,0:T(2,128)S(1)}, f32[2,128]{1,0:T(2,128)}, u32[]{:S(2)}) copy-start(f32[2,128]{1,0:T(2,128)} %constant.84.clone.1) | copy-start | bytes 3076
  47.2 9.0 %all-to-all-start.4 = ((f32[4,4,2,4,128]{4,3,2,1,0:T(4,128)}), f32[4,4,2,4,128]{4,3,2,1,0:T(4,128)S(1)}, u32[]{:S(2)}, u32[]{:S(2)}) async-start(f32[4,4,2,4,128]{4,3,2,1,0:T(4,128)} %copy.326), calls=%async_computation.4 | async-start | bytes 131072 | tf_op jit(solution)/shard_map/all_to_all | solution.py:220
  56.2 1.9 %collective-permute-start = (f32[4,1,2,4,128]{4,3,2,0,1:T(4,128)S(1)}, f32[4,1,2,4,128]{4,3,2,0,1:T(4,128)S(1)}, u32[]{:S(2)}, u32[]{:S(2)}) collective-permute-start(f32[4,1,2,4,128]{4,3,2,0,1:T(4,128)S(1)} %get-tuple-element.22), channel_id=1, source_target_pairs={{0,1},{1,0},{2,3},{3,2},{4,5},{5,4},{6,7},{7,6},{8,9},{9,8},{10,11... | collective-permute-start | bytes 49160 | tf_op jit(solution)/shard_map/ppermute | solution.py:48
  56.3 3.8 %collective-permute-start.1 = (f32[4,1,2,4,128]{4,3,2,0,1:T(4,128)S(1)}, f32[4,1,2,4,128]{4,3,2,0,1:T(4,128)S(1)}, u32[]{:S(2)}, u32[]{:S(2)}) collective-permute-start(f32[4,1,2,4,128]{4,3,2,0,1:T(4,128)S(1)} %get-tuple-element.21), channel_id=1, source_target_pairs={{0,2},{1,3},{2,0},{3,1},{4,6},{5,7},{6,4},{7,5},{8,10},{9,11},{10,... | collective-permute-start | bytes 49160 | tf_op jit(solution)/shard_map/ppermute | solution.py:48
  56.4 3.7 %collective-permute-start.2 = (f32[4,1,2,4,128]{4,3,2,0,1:T(4,128)S(1)}, f32[4,1,2,4,128]{4,3,2,0,1:T(4,128)S(1)}, u32[]{:S(2)}, u32[]{:S(2)}) collective-permute-start(f32[4,1,2,4,128]{4,3,2,0,1:T(4,128)S(1)} %get-tuple-element.23), channel_id=1, source_target_pairs={{0,3},{1,2},{2,1},{3,0},{4,7},{5,6},{6,5},{7,4},{8,11},{9,10},{10,... | collective-permute-start | bytes 49160 | tf_op jit(solution)/shard_map/ppermute | solution.py:48
